TPU v7x, 512 devices: a whole 4x8x8 slice. The times are simulated.
512 devices in a mesh: seq: 128 (over x, z_hi, y), tp: 4 (over z_lo, core).
Axes of the slice: x: 4, y: 8, z: 8 (z_hi: 4, z_lo: 2; z = z_hi * 2 + z_lo), core: 2. Of those that a mesh axis runs over, the one named last changes fastest.
Arguments:
- queries: bfloat16 [16384, 4096], P('seq', 'tp'), may hold values from -16 to 16
- keyvalues: bfloat16 [2, 16384, 1024], P(None, 'seq', 'tp'), may hold values from -16 to 16
- stretch_order: int32 [128], replicated, may hold values from 0 to 127, each once
- block_table: int32 [128, 128], replicated, may hold values 0 or 1
- proj_weight: bfloat16 [4096, 2048], P('tp'), may hold values from -0.09375 to 0.09375
Outputs:
- projected: bfloat16 [16384, 2048], P('seq', 'tp')
Inputs may be any that keep to these rules, and one draw needn't show every extreme that they name: `stretch_order`: every stretch number 0 to 127 appears once. `block_table`: entry [i, j] matters only where j < i.
All inputs are finite; a program needn't handle non-finite values.
Results may differ from a plain program's by a relative error of at most 0.014.
Values may be sent and summed in bfloat16 or wider, within the bound.
No kernel may reach another device: no remote copies, remote signals or barrier semaphores. Data moves between devices by JAX's collectives and lax.ppermute only.
A program may use at most 128 MiB of HBM per device.

v0:
```python
import math

import jax
import jax.numpy as jnp
from jax import lax
from jax.sharding import PartitionSpec as P

HEAD_SIZE = 128


def side_by_side(arrays, axis, dim, along):
    widths = [a.shape[along] for a in arrays]
    both = jnp.concatenate(arrays, axis=along)
    filled = lax.all_gather(both, axis, axis=dim, tiled=True)
    return tuple(jnp.split(filled, [sum(widths[:k]) for k in range(1, len(widths))], axis=along))


def cut_along(shard, dim, count):
    lengths = shard.shape
    blocks = shard.reshape(*lengths[:dim], count, lengths[dim] // count, *lengths[dim + 1 :])
    return jnp.moveaxis(blocks, dim, 0)


def sum_at_owner(shard, axis, dim):
    count = lax.axis_size(axis)
    blocks = lax.all_to_all(cut_along(shard, dim, count), axis, 0, 0, tiled=True)
    return jnp.sum(blocks.astype(jnp.float32), axis=0)


def per_device(queries, keyvalues, stretch_order, block_table, proj_weight):
    shard_rows = queries.shape[0]
    kv_width = keyvalues.shape[2]
    kv_heads = kv_width // HEAD_SIZE
    q_heads = queries.shape[1] // HEAD_SIZE
    group_width = q_heads // kv_heads
    stretch_total = stretch_order.shape[0]
    score_scale = 1.0 / HEAD_SIZE**0.5
    my_index = lax.axis_index("seq")
    my_stretch = stretch_order[my_index]
    table_row = block_table[my_stretch]
    query_pos = my_stretch * shard_rows + jnp.arange(shard_rows, dtype=jnp.int32)
    query_four = queries.reshape(shard_rows, kv_heads, group_width, HEAD_SIZE)
    stretch_ids = jnp.arange(stretch_total, dtype=jnp.int32)

    def attend(carried, key_matrix, value_matrix, key_stretches):
        row_count = key_matrix.shape[0]
        key_pos = key_stretches * shard_rows + jnp.arange(row_count, dtype=jnp.int32) % shard_rows
        table_hits = jnp.sum(
            jnp.where(key_stretches[:, None] == stretch_ids[None, :], table_row[None, :], 0), axis=1
        )
        same_stretch = (key_stretches[None, :] == my_stretch) & (
            key_pos[None, :] <= query_pos[:, None]
        )
        earlier = (key_stretches[None, :] < my_stretch) & (table_hits[None, :] == 1)
        allowed = same_stretch | earlier
        scores = (
            jnp.einsum(
                "tkgd,skd->kgts",
                query_four,
                key_matrix.reshape(row_count, kv_heads, HEAD_SIZE),
                preferred_element_type=jnp.float32,
            )
            * score_scale
        )
        scores = jnp.where(allowed, scores, -1e30)
        running_max, denominator, numerator = carried
        new_max = jnp.maximum(running_max, jnp.max(scores, axis=-1))
        weights = jnp.where(allowed, jnp.exp(scores - new_max[..., None]), 0.0)
        factor = jnp.exp(running_max - new_max)
        denominator = denominator * factor + jnp.sum(weights, axis=-1)
        numerator = numerator * factor[..., None] + jnp.einsum(
            "kgts,skd->kgtd",
            weights.astype(jnp.bfloat16),
            value_matrix.reshape(row_count, kv_heads, HEAD_SIZE),
            preferred_element_type=jnp.float32,
        )
        return (new_max, denominator, numerator)

    start_state = (
        jnp.full((kv_heads, group_width, shard_rows), -1e30, jnp.float32),
        jnp.zeros((kv_heads, group_width, shard_rows), jnp.float32),
        jnp.zeros((kv_heads, group_width, shard_rows, HEAD_SIZE), jnp.float32),
    )
    piece = side_by_side((keyvalues[0], keyvalues[1]), "seq", 0, 1)
    key_matrix = piece[0]
    value_matrix = piece[1]
    shard_count = key_matrix.shape[0] // shard_rows
    grouped = math.gcd(shard_count, max(1, 512 // shard_rows))
    span_rows = shard_rows * grouped

    def many_shards(block_index, inner):
        sources = block_index * grouped + jnp.arange(span_rows, dtype=jnp.int32) // shard_rows
        stretches = jnp.sum(
            jnp.where(sources[:, None] == stretch_ids[None, :], stretch_order[None, :], 0), axis=1
        )
        block_keys = lax.dynamic_slice_in_dim(key_matrix, block_index * span_rows, span_rows, 0)
        block_values = lax.dynamic_slice_in_dim(value_matrix, block_index * span_rows, span_rows, 0)
        return attend(inner, block_keys, block_values, stretches)

    final = lax.fori_loop(0, shard_count // grouped, many_shards, start_state)
    running_max, denominator, numerator = final
    attended = numerator / denominator[..., None]
    attended = (
        jnp.transpose(attended, (2, 0, 1, 3))
        .reshape(shard_rows, q_heads * HEAD_SIZE)
        .astype(jnp.bfloat16)
    )
    partial_sums = jnp.dot(attended, proj_weight, preferred_element_type=jnp.float32)
    return sum_at_owner(partial_sums.astype(jnp.bfloat16), "tp", 1).astype(jnp.bfloat16)


def solution(mesh):
    in_specs = (P("seq", "tp"), P(None, "seq", "tp"), P(), P(), P("tp", None))
    out_specs = P("seq", "tp")
    return jax.shard_map(
        per_device, mesh=mesh, in_specs=in_specs, out_specs=out_specs, check_vma=False
    )
```

profile of v0, /device:TPU:1, one launch (start us, length us, event | category | flops | bytes accessed | tf_op | source)
XLA Modules:
  0.0 459.1 jit_solution(548936549895772356)
XLA Ops:
  8.4 1.3 dynamic_slice.26
  11.8 1.1 copy.29
  13.8 263.0 %all-gather.2.cloned.1.call-done = bf16[16384,512]{0,1:T(8,128)(2,1)} async-done(((bf16[128,512]{0,1:T(8,128)(2,1)}), bf16[16384,512]{0,1:T(8,128)(2,1)}) %all-gather.2.cloned.1.call-update) | async-done | bytes 16777232 | tf_op jit(solution)/shard_map/all_gather | solution.py:14
  276.8 11.4 %fusion.25 = (bf16[16384,256]{0,1:T(8,128)(2,1)}, bf16[16384,256]{0,1:T(8,128)(2,1)}) fusion(bf16[16384,512]{0,1:T(8,128)(2,1)} %all-gather.2.cloned.1.call-done), kind=kLoop, calls=%fused_computation.48 | loop fusion | bytes 33554432 | tf_op jit(solution)/shard_map/split | solution.py:15
  288.3 148.5 %while.21 = (s32[]{:T(128)}, f32[2,4,128]{2,1,0:T(4,128)S(1)}, f32[2,4,128]{2,1,0:T(4,128)S(1)}, f32[2,4,128,128]{3,2,1,0:T(8,128)S(1)}, s32[128]{0:T(128)S(1)},...) while((s32[]{:T(128)}, f32[2,4,128]{2,1,0:T(4,128)S(1)}, ...), condition=%wide.region_5.6_spmd.clone.clone, body=%wide.region_0.5_spmd.clone.clone.sunk | while | flops 276249216 | bytes 9527531 | solution.py:100
  289.8 1.1 constant_dynamic-slice_fusion.4
  291.9 0.9 convolution_add_fusion.2
  294.4 1.1 constant_dynamic-slice_fusion.4
  296.6 0.9 convolution_add_fusion.2
  299.0 1.1 constant_dynamic-slice_fusion.4
  301.2 0.9 convolution_add_fusion.2
  303.7 1.1 constant_dynamic-slice_fusion.4
  305.8 0.9 convolution_add_fusion.2
  308.3 1.1 constant_dynamic-slice_fusion.4
  310.5 0.9 convolution_add_fusion.2
  312.9 1.1 constant_dynamic-slice_fusion.4
  315.1 0.9 convolution_add_fusion.2
  317.6 1.1 constant_dynamic-slice_fusion.4
  319.8 0.9 convolution_add_fusion.2
  322.2 1.1 constant_dynamic-slice_fusion.4
  324.4 0.9 convolution_add_fusion.2
  326.9 1.1 constant_dynamic-slice_fusion.4
  329.0 0.9 convolution_add_fusion.2
  331.5 1.1 constant_dynamic-slice_fusion.4
  333.7 0.9 convolution_add_fusion.2
  336.1 1.1 constant_dynamic-slice_fusion.4
  338.3 0.9 convolution_add_fusion.2
  340.8 1.1 constant_dynamic-slice_fusion.4
  343.0 0.9 convolution_add_fusion.2
  345.4 1.1 constant_dynamic-slice_fusion.4
  347.6 0.9 convolution_add_fusion.2
  350.1 1.1 constant_dynamic-slice_fusion.4
  352.3 0.9 convolution_add_fusion.2
  354.7 1.1 constant_dynamic-slice_fusion.4
  356.9 0.9 convolution_add_fusion.2
  359.3 1.1 constant_dynamic-slice_fusion.4
  361.5 0.9 convolution_add_fusion.2
  364.0 1.1 constant_dynamic-slice_fusion.4
  366.2 0.9 convolution_add_fusion.2
  368.6 1.1 constant_dynamic-slice_fusion.4
  373.3 1.1 constant_dynamic-slice_fusion.4
  375.5 0.9 convolution_add_fusion.2
  377.9 1.1 constant_dynamic-slice_fusion.4
  380.1 0.9 convolution_add_fusion.2
  382.6 1.1 constant_dynamic-slice_fusion.4
  387.2 1.1 constant_dynamic-slice_fusion.4
  389.4 0.9 convolution_add_fusion.2
  391.8 1.1 constant_dynamic-slice_fusion.4
  396.5 1.1 constant_dynamic-slice_fusion.4
  401.1 1.1 constant_dynamic-slice_fusion.4
  403.3 0.9 convolution_add_fusion.2
  405.8 1.1 constant_dynamic-slice_fusion.4
  407.9 0.9 convolution_add_fusion.2
  410.4 1.1 constant_dynamic-slice_fusion.4
  415.0 1.1 constant_dynamic-slice_fusion.4
  417.2 0.9 convolution_add_fusion.2
  419.7 1.1 constant_dynamic-slice_fusion.4
  424.3 1.1 constant_dynamic-slice_fusion.4
  428.9 1.1 constant_dynamic-slice_fusion.4
  431.1 0.9 convolution_add_fusion.2
  433.6 1.1 constant_dynamic-slice_fusion.4
  435.8 0.9 convolution_add_fusion.2
  437.0 2.9 convolution_convert_fusion
  440.0 11.6 %all_to_all.5 = bf16[4,128,512]{2,1,0:T(8,128)(2,1)S(1)} all-to-all(bf16[4,128,512]{2,1,0:T(8,128)(2,1)S(1)} %bitcast.62), channel_id=1, replica_groups=mesh['seq'=128,'tp'=4] {'tp'}, dimensions={0} | all-to-all | bytes 1048576 | tf_op jit(solution)/shard_map/all_to_all | solution.py:26
  (410 shorter events, 90.6 us)
Async XLA Ops:
  6.5 7.2 %copy-start = (s32[128,128]{1,0:T(8,128)S(1)}, s32[128,128]{1,0:T(8,128)}, u32[]{:S(2)}) copy-start(s32[128,128]{1,0:T(8,128)} %param.10) | copy-start | bytes 196612
  6.5 270.3 %all-gather.2.cloned.1.call-start = ((), (), s32[]{:S(2)}) async-start(), calls=%async_computation.1 | async-start | bytes 16908288 | tf_op jit(solution)/shard_map/all_gather | solution.py:14
  13.8 274.5 %copy-start.1 = (s32[128]{0:T(128)S(1)}, s32[128]{0:T(128)}, u32[]{:S(2)}) copy-start(s32[128]{0:T(128)} %param.9) | copy-start | bytes 1540
Sparse Core Ops, SparseCore 0:
  11.8 265.0 all-gather.1
where the time goes:
time: 460 us; the launch traced here: 459 us
  waiting for transfers between devices  263 us (57%)
  other arithmetic  65 us (14%)
  matrix products  50.5 us (11%)
  local copies, waits for them, and re-layouts  49.8 us (11%)
  between operations  16.2 us (4%)
  blocking collectives  11.6 us (3%)
    all_gather x1, waiting for transfers between devices, side_by_side(): filled = lax.all_gather(both, axis, axis=dim, tiled=True)  263 us
    dynamic_slice x32, local copies, waits for them, and re-layouts, many_shards(): lax.dynamic_slice_in_dim(value_matrix, block_index * span_rows, span_rows...  34.3 us
    dot_general x32, matrix products, attend(): jnp.einsum('kgts,skd->kgtd', weights.astype(jnp.bfloat16), value_matrix.r...  30.3 us
    eq x32, other arithmetic, attend(): key_stretches[None, :] == my_stretch  21.8 us
    dot_general x32, matrix products, attend(): jnp.einsum('tkgd,skd->kgts', query_four, key_matrix.reshape(row_count, kv...  17.3 us
    reduce_sum x32, other arithmetic, attend(): denominator = denominator * factor + jnp.sum(weights, axis=-1)  16.7 us
    all_to_all x1, blocking collectives, sum_at_owner(): lax.all_to_all(cut_along(shard, dim, count), axis, 0, 0, tiled=True)  11.6 us
    split x1, local copies, waits for them, and re-layouts, side_by_side(): jnp.split(filled, [sum(widths[:k]) for k in range(1, len(widths))], axis=...  11.4 us
  transfers between devices with their start and end apart: 1, of which 1 were waited for; matrix products, arithmetic and copies ran while one was open for 1% of the time, Pallas kernels for 0%

commit v1 on v0

v1 whole, which is shorter than its diff:
```python
import functools

import jax
import jax.numpy as jnp
from jax import lax
from jax.experimental import pallas as pl
from jax.experimental.pallas import tpu as pltpu
from jax.sharding import PartitionSpec as P


HEAD = 128
ROWS = 128
NX, NZ, NY = 4, 4, 8
SCALE2 = 1.4426950408889634 / HEAD**0.5
NEG = -1e30
KEYS = 4


SMEM = pl.BlockSpec(memory_space=pltpu.SMEM)
VMEM = pl.BlockSpec(memory_space=pltpu.VMEM)
PARAMS = pltpu.CompilerParams(vmem_limit_bytes=26 * 1024 * 1024)


def _shift(a, dx=0, dz=0, dy=0):
    pairs = []
    for x in range(NX):
        for z in range(NZ):
            for y in range(NY):
                src = (x * NZ + z) * NY + y
                dst = (((x + dx) % NX) * NZ + (z + dz) % NZ) * NY + (y + dy) % NY
                pairs.append((src, dst))
    return lax.ppermute(a, "seq", pairs)


X_GROUPS = [[x * NZ * NY + r for x in range(NX)] for r in range(NZ * NY)]
Z_GROUPS = [[(x * NZ + z) * NY + y for z in range(NZ)] for x in range(NX) for y in range(NY)]


def _swap(a, groups):
    return lax.all_to_all(a, "seq", 0, 0, tiled=True, axis_index_groups=groups)


def _flags_kernel(at_ref, order_ref, table_ref, out_ref):
    me = at_ref[0]
    x = lax.shift_right_logical(me, 5)
    z = lax.shift_right_logical(me, 3) & 3
    y = me & 7
    for j in range(NX):
        cq = order_ref[((x + j) & 3) * 32 + z * 8 + y]
        for n in range(NZ):
            base = x * 32 + n * 8
            for d in range(NY):
                ck = order_ref[base + ((y + d) & 7)]
                seen = jnp.where((ck < cq) & (table_ref[cq, ck] == 1), 1, 0)
                if j == 0 and d == 0:
                    seen = jnp.where(n == z, 2, seen)
                out_ref[j * 32 + d * 4 + n] = seen
    out_ref[128] = x


def _flags(order, table):
    me = lax.axis_index("seq").astype(jnp.int32).reshape(1)
    return pl.pallas_call(
        _flags_kernel,
        in_specs=[SMEM, SMEM, SMEM],
        out_specs=SMEM,
        out_shape=jax.ShapeDtypeStruct((NX * 32 + 1,), jnp.int32),
        name="flags",
    )(me, order, table)


def _unit(q_ref, i, kv_ref, base, bias, acc_ref, m_ref, j):
    scores = []
    for g in range(2):
        q = jnp.concatenate([q_ref[i, :, (g * 4 + h) * HEAD : (g * 4 + h + 1) * HEAD] for h in range(4)], axis=0)
        k = kv_ref[pl.ds(base, KEYS), :ROWS, g * HEAD : (g + 1) * HEAD].reshape(KEYS * ROWS, HEAD)
        scores.append(lax.dot_general(q, k, (((1,), (1,)), ((), ())), preferred_element_type=jnp.float32))
    for g in range(2):
        v = kv_ref[pl.ds(base, KEYS), ROWS:, g * HEAD : (g + 1) * HEAD].reshape(KEYS * ROWS, HEAD)
        v = jnp.concatenate([v, jnp.ones_like(v)], axis=1)
        s = scores[g] * SCALE2 + bias
        heads = slice(g * 4, g * 4 + 4)
        m_old = m_ref[j, heads].reshape(4 * ROWS, HEAD)
        m_new = jnp.maximum(m_old, jnp.max(s, axis=1, keepdims=True))
        p = jnp.exp2(s - jnp.concatenate([m_new] * KEYS, axis=1))
        pv = jnp.dot(p.astype(jnp.bfloat16), v, preferred_element_type=jnp.float32)
        factor = jnp.exp2(m_old - m_new)
        acc = acc_ref[j, heads].reshape(4 * ROWS, 2 * HEAD)
        acc = acc * jnp.concatenate([factor, factor], axis=1) + pv
        acc_ref[j, heads] = acc.reshape(4, ROWS, 2 * HEAD)
        m_ref[j, heads] = m_new.reshape(4, ROWS, HEAD)


def _finish(acc_ref, m_ref, j, out_ref, i):
    col = lax.broadcasted_iota(jnp.int32, (ROWS, HEAD), 1) % 8
    sums = jnp.zeros((ROWS, HEAD), jnp.float32)
    tops = jnp.zeros((ROWS, HEAD), jnp.float32)
    for h in range(8):
        total = acc_ref[j, h, :, HEAD:]
        safe = jnp.where(total > 0.0, total, 1.0)
        out_ref[i, :, h * HEAD : (h + 1) * HEAD] = (acc_ref[j, h, :, :HEAD] / safe).astype(jnp.bfloat16)
        sums = jnp.where(col == h, total, sums)
        tops = jnp.where(col == h, m_ref[j, h], tops)
    some = sums > 0.0
    ext = jnp.where(some, tops + jnp.log2(jnp.where(some, sums, 1.0)), NEG)
    col = lax.broadcasted_iota(jnp.int32, (ROWS, HEAD), 1)
    hi = ext.astype(jnp.bfloat16).astype(jnp.float32)
    left = ext - hi
    mid = left.astype(jnp.bfloat16).astype(jnp.float32)
    ext = jnp.where(col < 8, hi, jnp.where(col < 16, mid, left - mid))
    out_ref[i, :, 8 * HEAD :] = ext.astype(jnp.bfloat16)


def _attend_kernel(*refs, dists, queries, first, last):
    nq, nc = len(queries), len(dists)
    own = queries == (0,)
    flag_ref, q_ref = refs[:2]
    chunk_refs = refs[2 : 2 + nc]
    rest = list(refs[2 + nc :])
    state = [] if first else [rest.pop(0), rest.pop(0)]
    kv_ref = rest.pop()
    if last:
        out_ref = rest.pop(0)
    acc_ref, m_ref = rest
    for c, ref in enumerate(chunk_refs):
        kv_ref[c * NZ : (c + 1) * NZ] = ref[...]
    if first:
        acc_ref[...] = jnp.zeros_like(acc_ref)
        m_ref[...] = jnp.full_like(m_ref, NEG)
    else:
        acc_ref[...] = state[0][...]
        m_ref[...] = state[1][...]
    lane = lax.broadcasted_iota(jnp.int32, (1, KEYS * ROWS), 1) // ROWS
    x = flag_ref[NX * 32]

    def where_q(j):
        return 0 if own else (x + queries[0] + j) & 3

    def run(j, c, masked):
        at = dists[0]
        for k in range(1, nc):
            at = jnp.where(c == k, dists[k], at)
        flags = [flag_ref[(queries[0] + j) * 32 + at * 4 + n] for n in range(KEYS)]

        @pl.when(functools.reduce(jnp.maximum, flags) > 0)
        def _():
            bias = jnp.full((1, KEYS * ROWS), NEG, jnp.float32)
            for n, f in enumerate(flags):
                bias = jnp.where((lane == n) & (f > 0), 0.0, bias)
            if masked:
                same = jnp.zeros((1, KEYS * ROWS), jnp.float32)
                for n, f in enumerate(flags):
                    same = jnp.where((lane == n) & (f == 2), 1.0, same)
                key = lax.broadcasted_iota(jnp.int32, (ROWS, KEYS * ROWS), 1) % ROWS
                row = lax.broadcasted_iota(jnp.int32, (ROWS, KEYS * ROWS), 0)
                bias = bias + jnp.where(key > row, NEG, 0.0) * same
                bias = jnp.concatenate([bias] * 4, axis=0)
            _unit(q_ref, where_q(j), kv_ref, c * NZ, bias, acc_ref, m_ref, j)

    if own:
        run(0, 0, True)

    def each(u, carry):
        if nq == 1:
            run(0, u, False)
        elif nc == 1:
            run(u, 0, False)
        else:
            run(u // nc, u % nc, False)
        return carry

    lax.fori_loop(1 if own else 0, nq * nc, each, 0)
    if last:
        for j in range(nq):
            _finish(acc_ref, m_ref, j, out_ref, where_q(j))


def _attend(flags, q, chunks, dists, state, last, queries):
    nq, nc = len(queries), len(chunks)
    first = state is None
    args = [flags, q, *chunks] + ([] if first else list(state))
    acc = jax.ShapeDtypeStruct((nq, 8, ROWS, 2 * HEAD), jnp.float32)
    top = jax.ShapeDtypeStruct((nq, 8, ROWS, HEAD), jnp.float32)
    scratch = [pltpu.VMEM((nc * NZ, 2 * ROWS, 2 * HEAD), jnp.bfloat16)]
    if last:
        out = (jax.ShapeDtypeStruct((q.shape[0], ROWS, 9 * HEAD), jnp.bfloat16),)
        scratch = [pltpu.VMEM(acc.shape, acc.dtype), pltpu.VMEM(top.shape, top.dtype)] + scratch
    else:
        out = (acc, top)
    pairs = nq * nc * NZ * 8
    got = pl.pallas_call(
        functools.partial(_attend_kernel, dists=dists, queries=queries, first=first, last=last),
        in_specs=[SMEM] + [VMEM] * (len(args) - 1),
        out_specs=tuple(VMEM for _ in out),
        out_shape=out,
        scratch_shapes=scratch,
        compiler_params=PARAMS,
        cost_estimate=pl.CostEstimate(
            flops=pairs * ROWS * ROWS * HEAD * 4, transcendentals=pairs * ROWS * ROWS, bytes_accessed=4 << 20
        ),
    )(*args)
    return got[0] if last else got


def _combine_kernel(at_ref, flag_ref, own_ref, part_ref, w_ref, att_ref, out_ref):
    x = flag_ref[NX * 32]
    lses = []
    for j in range(NX):
        ext = own_ref[0, :, 8 * HEAD :] if j == 0 else part_ref[(x + j) & 3, :, 8 * HEAD :]
        ext = ext.astype(jnp.float32)
        lses.append(ext[:, 0:8] + ext[:, 8:16] + ext[:, 16:24])
    top = functools.reduce(jnp.maximum, lses)
    ws = [jnp.exp2(v - top) for v in lses]
    total = functools.reduce(jnp.add, ws)
    ws = [w / total for w in ws]
    for h in range(8):
        at = slice(h * HEAD, (h + 1) * HEAD)
        mixed = ws[0][:, h : h + 1] * own_ref[0, :, at].astype(jnp.float32)
        for j in range(1, NX):
            mixed += ws[j][:, h : h + 1] * part_ref[(x + j) & 3, :, at].astype(jnp.float32)
        att_ref[:, at] = mixed.astype(jnp.bfloat16)
    _columns(at_ref, att_ref, w_ref, out_ref, 1)


def _columns(at_ref, att_ref, w_ref, out_ref, flip):
    me = at_ref[0]
    for n in range(2):
        at = pl.multiple_of((me ^ (2 * n + flip)) * 512, 512)
        out_ref[n] = jnp.dot(
            att_ref[...], w_ref[:, pl.ds(at, 512)], preferred_element_type=jnp.float32
        ).astype(out_ref.dtype)


def _keep_kernel(at_ref, att_ref, w_ref, out_ref):
    _columns(at_ref, att_ref, w_ref, out_ref, 0)


def _call(kernel, args, out, flops):
    many = isinstance(out, tuple)
    return pl.pallas_call(
        kernel,
        in_specs=[SMEM if a.dtype == jnp.int32 else VMEM for a in args],
        out_specs=tuple(VMEM for _ in out) if many else VMEM,
        out_shape=out,
        compiler_params=PARAMS,
        cost_estimate=pl.CostEstimate(flops=flops, transcendentals=0, bytes_accessed=5 << 20),
    )(*args)


def _ring(a, dy):
    return _shift(a, dy=dy)


def per_device(queries, keyvalues, stretch_order, block_table, proj_weight):
    kv = keyvalues.reshape(1, 2 * ROWS, 2 * HEAD)
    near = _swap(jnp.broadcast_to(kv, (NZ, 2 * ROWS, 2 * HEAD)), Z_GROUPS)
    q = _swap(jnp.broadcast_to(queries[None], (NX, ROWS, 8 * HEAD)), X_GROUPS)
    flags = _flags(stretch_order, block_table)
    others = (1, 2, 3)
    f1, b1 = _ring(near, 1), _ring(near, -1)
    f2, b2 = _ring(f1, 1), _ring(b1, -1)
    state = _attend(flags, q, [near, f1, b1], (0, 7, 1), None, False, others)
    f3, b3 = _ring(f2, 1), _ring(b2, -1)
    state = _attend(flags, q, [f2, b2], (6, 2), state, False, others)
    f4, b4 = _ring(f3[:2], 1), _ring(b3[2:], -1)
    state = _attend(flags, q, [f3, b3], (5, 3), state, False, others)
    far = jnp.concatenate([f4, b4], axis=0)
    parts = _attend(flags, q, [far], (4,), state, True, others)
    parts = _swap(parts, X_GROUPS)
    chunks = [near, f1, b1, f2, b2, f3, b3, far]
    own = _attend(flags, queries[None], chunks, (0, 7, 1, 6, 2, 5, 3, 4), None, True, (0,))
    me = lax.axis_index("tp").astype(jnp.int32).reshape(1)
    att, give = _call(
        _combine_kernel,
        [me, flags, own, parts, proj_weight],
        (jax.ShapeDtypeStruct((ROWS, 8 * HEAD), jnp.bfloat16), jax.ShapeDtypeStruct((2, ROWS, 512), jnp.bfloat16)),
        2 * ROWS * 1024 * 1024,
    )
    took = lax.ppermute(give, "tp", [(t, t ^ 1) for t in range(4)])
    keep = _call(
        _keep_kernel, [me, att, proj_weight], jax.ShapeDtypeStruct((2, ROWS, 512), jnp.float32), 2 * ROWS * 1024 * 1024
    )
    both = keep + took.astype(jnp.float32)
    beside = lax.ppermute(both[1].astype(jnp.bfloat16), "tp", [(t, t ^ 2) for t in range(4)])
    return (both[0] + beside.astype(jnp.float32)).astype(jnp.bfloat16)


def solution(mesh):
    in_specs = (P("seq", "tp"), P(None, "seq", "tp"), P(), P(), P("tp", None))
    return jax.shard_map(
        per_device, mesh=mesh, in_specs=in_specs, out_specs=P("seq", "tp"), check_vma=False
    )
```

time: 460 us -> 146 us (0.32)
  waiting for transfers between devices: 263 us -> 14.4 us
  other arithmetic: 65 us -> 0.75 us
  starting transfers between devices: 0.01 us -> 57 us
  matrix products: 50.5 us -> 0 us
  local copies, waits for them, and re-layouts: 49.8 us -> 11.9 us
  Pallas kernels: 0 us -> 36.4 us
  between operations: 16.2 us -> 0.29 us
  blocking collectives: 11.6 us -> 24 us
    all_gather x1 -> x0, waiting for transfers between devices: 263 us -> none  [side_by_side(): filled = lax.all_gather(both, axis, axis=dim, tiled=True)]
    dot_general x65 -> x0, matrix products: 50.5 us -> none  [the longest x32 30.3 us: attend(): jnp.einsum('kgts,skd->kgtd', weights.astype(jnp.bfloat16), value_matrix.r...]
    ppermute x0 -> x10, starting transfers between devices: none -> 46 us  [the longest x8 28 us: _shift(): return lax.ppermute(a, 'seq', pairs)]
    pallas_call x0 -> x8, Pallas kernels: none -> 36.4 us  [the longest x5 31.3 us: _attend(): pl.pallas_call(functools.partial(_attend_kernel, dists=dists, queries=que...]
    dynamic_slice x34 -> x0, local copies, waits for them, and re-layouts: 35.6 us -> none  [the longest x32 34.3 us: many_shards(): lax.dynamic_slice_in_dim(value_matrix, block_index * span_rows, span_rows...]
    reduce_sum x97 -> x0, other arithmetic: 32.5 us -> none  [the longest x32 16.7 us: attend(): denominator = denominator * factor + jnp.sum(weights, axis=-1)]
    eq x32 -> x0, other arithmetic: 21.8 us -> none  [attend(): key_stretches[None, :] == my_stretch]
    ppermute x0 -> x10, waiting for transfers between devices: none -> 14.4 us  [the longest x8 10.3 us: _shift(): return lax.ppermute(a, 'seq', pairs)]
  transfers between devices with their start and end apart: 1 -> 12, of which waited for: 1 -> 4; matrix products, arithmetic and copies ran while one was open for 1% -> 1% of each run, Pallas kernels for 0% -> 20%
where the time goes in v1:
time: 146 us; the launch traced here: 145 us
  starting transfers between devices  57 us (39%)
  Pallas kernels  36.4 us (25%)
  blocking collectives  24 us (16%)
  waiting for transfers between devices  14.4 us (10%)
  local copies, waits for them, and re-layouts  11.9 us (8%)
    pallas_call x5, Pallas kernels, _attend(): pl.pallas_call(functools.partial(_attend_kernel, dists=dists, queries=que...  31.3 us
    ppermute x8, starting transfers between devices, _shift(): return lax.ppermute(a, 'seq', pairs)  28 us
    all_to_all x1, blocking collectives, _swap(): return lax.all_to_all(a, 'seq', 0, 0, tiled=True, axis_index_groups=groups)  24 us
    all_to_all x2, starting transfers between devices, _swap(): return lax.all_to_all(a, 'seq', 0, 0, tiled=True, axis_index_groups=groups)  11.1 us
    ppermute x1, starting transfers between devices, per_device(): took = lax.ppermute(give, 'tp', [(t, t ^ 1) for t in range(4)])  10.8 us
    ppermute x8, waiting for transfers between devices, _shift(): return lax.ppermute(a, 'seq', pairs)  10.3 us
    unnamed x31, local copies, waits for them, and re-layouts  9.78 us
    ppermute x1, starting transfers between devices, per_device(): lax.ppermute(both[1].astype(jnp.bfloat16), 'tp', [(t, t ^ 2) for t in ran...  7.12 us
  transfers between devices with their start and end apart: 12, of which 4 were waited for; matrix products, arithmetic and copies ran while one was open for 1% of the time, Pallas kernels for 20%

profile of v1, /device:TPU:1, one launch (start us, length us, event | category | flops | bytes accessed | tf_op | source)
XLA Modules:
  0.0 144.9 jit_solution(4238092858335345516)
XLA Ops:
  0.0 1.0 broadcast_in_dim.18
  1.0 24.0 %all_to_all.15.refs_2_ = bf16[4,256,256]{2,1,0:T(8,128)(2,1)S(1)} all-to-all(bf16[4,256,256]{2,1,0:T(8,128)(2,1)S(1)} %broadcast_in_dim.18), channel_id=1, replica_groups={{0,32,64,96},{4,36,68,100},{8,40,72,104},{12,44,76,108},{16,48,80,112},..., dimensions={0} | all-to-all | bytes 1048576 | tf_op jit(solution)/shard_map/all_to_all | solution.py:40
  25.0 0.0 copy-start.4
  25.0 3.2 %collective-permute-start = (bf16[4,256,256]{2,1,0:T(8,128)(2,1)S(1)}, bf16[4,256,256]{2,1,0:T(8,128)(2,1)S(1)}, u32[]{:S(2)}, u32[]{:S(2)}) collective-permute-start(bf16[4,256,256]{2,1,0:T(8,128)(2,1)S(1)} %all_to_all.15.refs_2_), channel_id=1, source_target_pairs={{0,4},{4,8},{8,12},{12,16},{16,20},{20,24},{24,28},{28,0},{32,36},... | collective-permute-start | bytes 1572872 | tf_op jit(solution)/shard_map/ppermute | solution.py:32
  28.2 3.8 %collective-permute-start.1 = (bf16[4,256,256]{2,1,0:T(8,128)(2,1)S(1)}, bf16[4,256,256]{2,1,0:T(8,128)(2,1)}, u32[]{:S(2)}, u32[]{:S(2)}) collective-permute-start(bf16[4,256,256]{2,1,0:T(8,128)(2,1)S(1)} %all_to_all.15.refs_2_), channel_id=1, source_target_pairs={{0,28},{4,0},{8,4},{12,8},{16,12},{20,16},{24,20},{28,24},{32,60},... | collective-permute-start | bytes 1572872 | tf_op jit(solution)/shard_map/ppermute | solution.py:32
  32.0 5.8 %collective-permute-done.refs_3_ = bf16[4,256,256]{2,1,0:T(8,128)(2,1)S(1)} collective-permute-done((bf16[4,256,256]{2,1,0:T(8,128)(2,1)S(1)}, bf16[4,256,256]{2,1,0:T(8,128)(2,1)S(1)}, u32[]{:S(2)}, u32[]{:S(2)}) %collective-permute-start) | collective-permute-done | bytes 524320 | tf_op jit(solution)/shard_map/ppermute | solution.py:32
  37.8 0.0 copy-start.12
  37.8 1.9 %collective-permute-start.2 = (bf16[4,256,256]{2,1,0:T(8,128)(2,1)S(1)}, bf16[4,256,256]{2,1,0:T(8,128)(2,1)S(1)}, u32[]{:S(2)}, u32[]{:S(2)}) collective-permute-start(bf16[4,256,256]{2,1,0:T(8,128)(2,1)S(1)} %collective-permute-done.refs_3_), channel_id=1, source_target_pairs={{0,4},{4,8},{8,12},{12,16},{16,20},{20,24},{24,28},{28,0},{32,36},... | collective-permute-start | bytes 1572872 | tf_op jit(solution)/shard_map/ppermute | solution.py:32
  39.7 0.0 copy-done.9
  39.7 1.1 broadcast_in_dim.19
  40.8 0.0 copy-done.4
  40.8 0.0 copy-done.12
  40.8 4.0 %all-to-all-start.1 = ((bf16[4,128,1024]{2,1,0:T(8,128)(2,1)}), bf16[4,128,1024]{2,1,0:T(8,128)(2,1)S(1)}, u32[]{:S(2)}, u32[]{:S(2)}) async-start(bf16[4,128,1024]{2,1,0:T(8,128)(2,1)} %broadcast_in_dim.19), calls=%async_computation.1 | async-start | bytes 2097152 | tf_op jit(solution)/shard_map/all_to_all | solution.py:40
  44.9 0.0 collective-permute-done.1.refs_4_
  44.9 4.6 %collective-permute-start.3 = (bf16[4,256,256]{2,1,0:T(8,128)(2,1)}, bf16[4,256,256]{2,1,0:T(8,128)(2,1)S(1)}, u32[]{:S(2)}, u32[]{:S(2)}) collective-permute-start(bf16[4,256,256]{2,1,0:T(8,128)(2,1)} %collective-permute-done.1.refs_4_), channel_id=1, source_target_pairs={{0,28},{4,0},{8,4},{12,8},{16,12},{20,16},{24,20},{28,24},{32,60},... | collective-permute-start | bytes 1572872 | tf_op jit(solution)/shard_map/ppermute | solution.py:32
  49.4 0.0 collective-permute-done.2.refs_5_.refs_2_
  49.4 1.9 %collective-permute-start.4 = (bf16[4,256,256]{2,1,0:T(8,128)(2,1)S(1)}, bf16[4,256,256]{2,1,0:T(8,128)(2,1)S(1)}, u32[]{:S(2)}, u32[]{:S(2)}) collective-permute-start(bf16[4,256,256]{2,1,0:T(8,128)(2,1)S(1)} %collective-permute-done.2.refs_5_.refs_2_), channel_id=1, source_target_pairs={{0,4},{4,8},{8,12},{12,16},{16,20},{20,24},{24,28},{28,0},{32,36},... | collective-permute-start | bytes 1572872 | tf_op jit(solution)/shard_map/ppermute | solution.py:32
  51.4 4.5 %collective-permute-done.3.refs_6_.refs_3_ = bf16[4,256,256]{2,1,0:T(8,128)(2,1)S(1)} collective-permute-done((bf16[4,256,256]{2,1,0:T(8,128)(2,1)}, bf16[4,256,256]{2,1,0:T(8,128)(2,1)S(1)}, u32[]{:S(2)}, u32[]{:S(2)}) %collective-permute-start.3) | collective-permute-done | bytes 524320 | tf_op jit(solution)/shard_map/ppermute | solution.py:32
  55.8 0.0 copy-start.2
  55.9 5.2 %collective-permute-start.5 = (bf16[4,256,256]{2,1,0:T(8,128)(2,1)S(1)}, bf16[4,256,256]{2,1,0:T(8,128)(2,1)S(1)}, u32[]{:S(2)}, u32[]{:S(2)}) collective-permute-start(bf16[4,256,256]{2,1,0:T(8,128)(2,1)S(1)} %collective-permute-done.3.refs_6_.refs_3_), channel_id=1, source_target_pairs={{0,28},{4,0},{8,4},{12,8},{16,12},{20,16},{24,20},{28,24},{32,60},... | collective-permute-start | bytes 1572872 | tf_op jit(solution)/shard_map/ppermute | solution.py:32
  61.1 2.8 %flags.1.refs_0_.flag_ref = s32[129]{0:T(256)} custom-call(s32[1]{0:T(128)} %bitcast.1.at_ref, s32[128]{0:T(128)} %order_ref.1, s32[128,128]{1,0:T(8,128)} %table_ref.1), custom_call_target="tpu_custom_call" | custom-call | tf_op jit(solution)/shard_map/flags/pallas_call | solution.py:63
  63.9 0.0 all-to-all-done.1.refs_1_
  63.9 0.0 copy-start.5
  63.9 1.0 copy-done.5
  64.9 0.0 copy-start.10
  64.9 0.7 copy-done.10
  65.6 0.0 copy-start.13
  65.6 1.0 copy-done.13
  66.7 8.4 %shard_map.56 = (f32[3,8,128,256]{3,2,1,0:T(8,128)S(1)}, f32[3,8,128,128]{3,2,1,0:T(8,128)S(1)}) custom-call(s32[129]{0:T(256)S(1)} %copy-done.10, bf16[4,128,1024]{2,1,0:T(8,128)(2,1)S(1)} %all-to-all-done.1.refs_1_, bf16[4,256,256]{2,1,0:T(8,128)(2,1)S(1)} %copy-done.5, bf16[4,256,256]{2,1,0:T(8,128)(2,1)S(1)} %copy-done.13, ...), custom_call_target="tpu_custom_call" | custom-call | flops 2415919104 | bytes 4194304 | tf_op jit(solution)/shard_map/pallas_call | solution.py:191
  75.1 0.0 collective-permute-done.4.refs_7_.refs_2_
  75.1 1.9 %collective-permute-start.6 = (bf16[2,256,256]{2,1,0:T(8,128)(2,1)S(1)}, bf16[2,256,256]{2,1,0:T(8,128)(2,1)S(1)}, u32[]{:S(2)}, u32[]{:S(2)}) collective-permute-start(bf16[2,256,256]{2,1,0:T(8,128)(2,1)S(1)} %slice.17), channel_id=1, source_target_pairs={{0,4},{4,8},{8,12},{12,16},{16,20},{20,24},{24,28},{28,0},{32,36},... | collective-permute-start | bytes 786440 | tf_op jit(solution)/shard_map/ppermute | solution.py:32
  77.0 0.0 copy-done.2
  77.0 4.9 %shard_map.57 = (f32[3,8,128,256]{3,2,1,0:T(8,128)S(1)}, f32[3,8,128,128]{3,2,1,0:T(8,128)S(1)}) custom-call(s32[129]{0:T(256)S(1)} %copy-done.10, bf16[4,128,1024]{2,1,0:T(8,128)(2,1)S(1)} %all-to-all-done.1.refs_1_, bf16[4,256,256]{2,1,0:T(8,128)(2,1)S(1)} %collective-permute-done.2.refs_5_.refs_2_, ...), custom_call_target="tpu_custom_call" | custom-call | flops 1610612736 | bytes 4194304 | tf_op jit(solution)/shard_map/pallas_call | solution.py:191
  81.9 0.0 collective-permute-done.5.refs_8_.refs_3_
  82.0 5.5 %collective-permute-start.7 = (bf16[2,256,256]{2,1,0:T(8,128)(2,1)S(1)}, bf16[2,256,256]{2,1,0:T(8,128)(2,1)S(1)}, u32[]{:S(2)}, u32[]{:S(2)}) collective-permute-start(bf16[2,256,256]{2,1,0:T(8,128)(2,1)S(1)} %slice.18), channel_id=1, source_target_pairs={{0,28},{4,0},{8,4},{12,8},{16,12},{20,16},{24,20},{28,24},{32,60},... | collective-permute-start | bytes 786440 | tf_op jit(solution)/shard_map/ppermute | solution.py:32
  87.5 3.9 %shard_map.58 = (f32[3,8,128,256]{3,2,1,0:T(8,128)S(1)}, f32[3,8,128,128]{3,2,1,0:T(8,128)S(1)}) custom-call(s32[129]{0:T(256)S(1)} %copy-done.10, bf16[4,128,1024]{2,1,0:T(8,128)(2,1)S(1)} %all-to-all-done.1.refs_1_, bf16[4,256,256]{2,1,0:T(8,128)(2,1)S(1)} %collective-permute-done.4.refs_7_.refs_2_, ...), custom_call_target="tpu_custom_call" | custom-call | flops 1610612736 | bytes 4194304 | tf_op jit(solution)/shard_map/pallas_call | solution.py:191
  91.5 0.0 collective-permute-done.6
  91.5 0.0 collective-permute-done.7
  91.5 5.1 %shard_map.59 = bf16[4,128,1152]{2,1,0:T(8,128)(2,1)} custom-call(s32[129]{0:T(256)S(1)} %copy-done.10, bf16[4,128,1024]{2,1,0:T(8,128)(2,1)S(1)} %all-to-all-done.1.refs_1_, bf16[4,256,256]{2,1,0:T(8,128)(2,1)S(1)} %constant_dynamic-update-slice_fusion.refs_9_.refs_2_, f32[3,8,128,256]{3,2,1,0:T(8,128)S(1)} %get-tuple-element.17.refs_3_, ...), custom_call_target="tpu_custom_call" | custom-call | flops 805306368 | bytes 4194304 | tf_op jit(solution)/shard_map/pallas_call | solution.py:191
  96.6 0.0 copy-start.11
  96.6 7.0 %all-to-all-start.2 = ((bf16[4,128,1152]{2,1,0:T(8,128)(2,1)}), bf16[4,128,1152]{2,1,0:T(8,128)(2,1)S(1)}, u32[]{:S(2)}, u32[]{:S(2)}) async-start(bf16[4,128,1152]{2,1,0:T(8,128)(2,1)} %shard_map.59), calls=%async_computation.2 | async-start | bytes 2359296 | tf_op jit(solution)/shard_map/all_to_all | solution.py:40
  103.7 0.0 copy-done.11
  103.7 0.0 copy-start.3
  103.7 1.0 copy-done.3
  104.7 1.0 copy-done.6
  105.8 0.0 copy-start.14
  105.8 1.0 copy-done.14
  106.8 9.0 %shard_map.55.own_ref = bf16[1,128,1152]{2,1,0:T(8,128)(2,1)S(1)} custom-call(s32[129]{0:T(256)S(1)} %copy-done.11, bf16[1,128,1024]{2,1,0:T(8,128)(2,1)S(1)} %bitcast.12, bf16[4,256,256]{2,1,0:T(8,128)(2,1)S(1)} %copy-done.6, bf16[4,256,256]{2,1,0:T(8,128)(2,1)S(1)} %copy-done.14, bf16[4,256,256]{2,1,0:T(8,128)(2,1)} %collective-permute-done.1.refs_4_, ...), custom_call_target="tpu_custom_call" | custom-call | flops 2147483648 | bytes 4194304 | tf_op jit(solution)/shard_map/pallas_call | solution.py:191
  115.8 0.0 copy-start.7
  115.8 0.7 copy-done.7
  116.5 0.0 all-to-all-done.2.part_ref
  116.5 0.0 copy-start
  116.5 2.2 %copy-done = bf16[1024,2048]{1,0:T(8,128)(2,1)S(1)} copy-done((bf16[1024,2048]{1,0:T(8,128)(2,1)S(1)}, bf16[1024,2048]{1,0:T(8,128)(2,1)}, u32[]{:S(2)}) %copy-start) | copy-done | bytes 4194328
  118.7 0.0 copy-start.8
  118.7 1.0 copy-done.8
  119.7 1.8 %shard_map.60 = (bf16[128,1024]{1,0:T(8,128)(2,1)S(1)}, bf16[2,128,512]{2,1,0:T(8,128)(2,1)S(1)}) custom-call(s32[1]{0:T(128)} %bitcast.at_ref, s32[129]{0:T(256)S(1)} %copy-done.11, bf16[1,128,1152]{2,1,0:T(8,128)(2,1)S(1)} %copy-done.8, bf16[4,128,1152]{2,1,0:T(8,128)(2,1)S(1)} %all-to-all-done.2.part_ref, bf16[1024,2048]{1,0:T(8,128)(2,1)S(1)} %copy-done), custom_call_target="tpu_custom_call" | custom-call | flops 268435456 | bytes 5242880 | tf_op jit(solution)/shard_map/pallas_call | solution.py:240
  121.5 10.8 %collective-permute-start.8 = (bf16[2,128,512]{2,1,0:T(8,128)(2,1)S(1)}, bf16[2,128,512]{2,1,0:T(8,128)(2,1)S(1)}, u32[]{:S(2)}, u32[]{:S(2)}) collective-permute-start(bf16[2,128,512]{2,1,0:T(8,128)(2,1)S(1)} %get-tuple-element.20), channel_id=1, source_target_pairs={{0,1},{1,0},{2,3},{3,2},{4,5},{5,4},{6,7},{7,6},{8,9},{9,8},{10,11... | collective-permute-start | bytes 786440 | tf_op jit(solution)/shard_map/ppermute | solution.py:279
  132.3 0.0 copy-done.1
  132.3 0.5 shard_map.61
  132.8 0.7 collective-permute-done.8
  133.5 0.1 convert_add_fusion
  133.6 7.1 %collective-permute-start.9 = (bf16[128,512]{1,0:T(8,128)(2,1)S(1)}, bf16[128,512]{1,0:T(8,128)(2,1)S(1)}, u32[]{:S(2)}, u32[]{:S(2)}) collective-permute-start(bf16[128,512]{1,0:T(8,128)(2,1)S(1)} %fusion.2), channel_id=1, source_target_pairs={{0,2},{1,3},{2,0},{3,1},{4,6},{5,7},{6,4},{7,5},{8,10},{9,11},{10,... | collective-permute-start | bytes 393224 | tf_op jit(solution)/shard_map/ppermute | solution.py:284
  140.7 3.5 %collective-permute-done.9 = bf16[128,512]{1,0:T(8,128)(2,1)S(1)} collective-permute-done((bf16[128,512]{1,0:T(8,128)(2,1)S(1)}, bf16[128,512]{1,0:T(8,128)(2,1)S(1)}, u32[]{:S(2)}, u32[]{:S(2)}) %collective-permute-start.9) | collective-permute-done | bytes 131104 | tf_op jit(solution)/shard_map/ppermute | solution.py:284
  144.2 0.7 fusion.1
  (8 shorter events, 0.1 us)
Async XLA Ops:
  0.0 39.7 %copy-start.9 = (bf16[128,1024]{1,0:T(8,128)(2,1)S(1)}, bf16[128,1024]{1,0:T(8,128)(2,1)}, u32[]{:S(2)}) copy-start(bf16[128,1024]{1,0:T(8,128)(2,1)} %param.5) | copy-start | bytes 786436
  25.0 15.9 %copy-start.4 = (bf16[4,256,256]{2,1,0:T(8,128)(2,1)}, bf16[4,256,256]{2,1,0:T(8,128)(2,1)S(1)}, u32[]{:S(2)}) copy-start(bf16[4,256,256]{2,1,0:T(8,128)(2,1)S(1)} %all_to_all.15.refs_2_) | copy-start | bytes 1572868
  25.0 12.8 %collective-permute-start = (bf16[4,256,256]{2,1,0:T(8,128)(2,1)S(1)}, bf16[4,256,256]{2,1,0:T(8,128)(2,1)S(1)}, u32[]{:S(2)}, u32[]{:S(2)}) collective-permute-start(bf16[4,256,256]{2,1,0:T(8,128)(2,1)S(1)} %all_to_all.15.refs_2_), channel_id=1, source_target_pairs={{0,4},{4,8},{8,12},{12,16},{16,20},{20,24},{24,28},{28,0},{32,36},... | collective-permute-start | bytes 1572872 | tf_op jit(solution)/shard_map/ppermute | solution.py:32
  28.2 16.7 %collective-permute-start.1 = (bf16[4,256,256]{2,1,0:T(8,128)(2,1)S(1)}, bf16[4,256,256]{2,1,0:T(8,128)(2,1)}, u32[]{:S(2)}, u32[]{:S(2)}) collective-permute-start(bf16[4,256,256]{2,1,0:T(8,128)(2,1)S(1)} %all_to_all.15.refs_2_), channel_id=1, source_target_pairs={{0,28},{4,0},{8,4},{12,8},{16,12},{20,16},{24,20},{28,24},{32,60},... | collective-permute-start | bytes 1572872 | tf_op jit(solution)/shard_map/ppermute | solution.py:32
  37.8 3.0 %copy-start.12 = (bf16[4,256,256]{2,1,0:T(8,128)(2,1)}, bf16[4,256,256]{2,1,0:T(8,128)(2,1)S(1)}, u32[]{:S(2)}) copy-start(bf16[4,256,256]{2,1,0:T(8,128)(2,1)S(1)} %collective-permute-done.refs_3_) | copy-start | bytes 1572868
  37.8 11.6 %collective-permute-start.2 = (bf16[4,256,256]{2,1,0:T(8,128)(2,1)S(1)}, bf16[4,256,256]{2,1,0:T(8,128)(2,1)S(1)}, u32[]{:S(2)}, u32[]{:S(2)}) collective-permute-start(bf16[4,256,256]{2,1,0:T(8,128)(2,1)S(1)} %collective-permute-done.refs_3_), channel_id=1, source_target_pairs={{0,4},{4,8},{8,12},{12,16},{16,20},{20,24},{24,28},{28,0},{32,36},... | collective-permute-start | bytes 1572872 | tf_op jit(solution)/shard_map/ppermute | solution.py:32
  40.8 23.0 %all-to-all-start.1 = ((bf16[4,128,1024]{2,1,0:T(8,128)(2,1)}), bf16[4,128,1024]{2,1,0:T(8,128)(2,1)S(1)}, u32[]{:S(2)}, u32[]{:S(2)}) async-start(bf16[4,128,1024]{2,1,0:T(8,128)(2,1)} %broadcast_in_dim.19), calls=%async_computation.1 | async-start | bytes 2097152 | tf_op jit(solution)/shard_map/all_to_all | solution.py:40
  44.9 11.0 %collective-permute-start.3 = (bf16[4,256,256]{2,1,0:T(8,128)(2,1)}, bf16[4,256,256]{2,1,0:T(8,128)(2,1)S(1)}, u32[]{:S(2)}, u32[]{:S(2)}) collective-permute-start(bf16[4,256,256]{2,1,0:T(8,128)(2,1)} %collective-permute-done.1.refs_4_), channel_id=1, source_target_pairs={{0,28},{4,0},{8,4},{12,8},{16,12},{20,16},{24,20},{28,24},{32,60},... | collective-permute-start | bytes 1572872 | tf_op jit(solution)/shard_map/ppermute | solution.py:32
  49.4 25.6 %collective-permute-start.4 = (bf16[4,256,256]{2,1,0:T(8,128)(2,1)S(1)}, bf16[4,256,256]{2,1,0:T(8,128)(2,1)S(1)}, u32[]{:S(2)}, u32[]{:S(2)}) collective-permute-start(bf16[4,256,256]{2,1,0:T(8,128)(2,1)S(1)} %collective-permute-done.2.refs_5_.refs_2_), channel_id=1, source_target_pairs={{0,4},{4,8},{8,12},{12,16},{16,20},{20,24},{24,28},{28,0},{32,36},... | collective-permute-start | bytes 1572872 | tf_op jit(solution)/shard_map/ppermute | solution.py:32
  55.8 21.2 %copy-start.2 = (bf16[4,256,256]{2,1,0:T(8,128)(2,1)}, bf16[4,256,256]{2,1,0:T(8,128)(2,1)S(1)}, u32[]{:S(2)}) copy-start(bf16[4,256,256]{2,1,0:T(8,128)(2,1)S(1)} %collective-permute-done.3.refs_6_.refs_3_) | copy-start | bytes 1572868
  55.9 26.1 %collective-permute-start.5 = (bf16[4,256,256]{2,1,0:T(8,128)(2,1)S(1)}, bf16[4,256,256]{2,1,0:T(8,128)(2,1)S(1)}, u32[]{:S(2)}, u32[]{:S(2)}) collective-permute-start(bf16[4,256,256]{2,1,0:T(8,128)(2,1)S(1)} %collective-permute-done.3.refs_6_.refs_3_), channel_id=1, source_target_pairs={{0,28},{4,0},{8,4},{12,8},{16,12},{20,16},{24,20},{28,24},{32,60},... | collective-permute-start | bytes 1572872 | tf_op jit(solution)/shard_map/ppermute | solution.py:32
  63.9 1.0 copy-start.5
  64.9 0.7 copy-start.10
  65.6 1.0 copy-start.13
  75.1 16.4 %collective-permute-start.6 = (bf16[2,256,256]{2,1,0:T(8,128)(2,1)S(1)}, bf16[2,256,256]{2,1,0:T(8,128)(2,1)S(1)}, u32[]{:S(2)}, u32[]{:S(2)}) collective-permute-start(bf16[2,256,256]{2,1,0:T(8,128)(2,1)S(1)} %slice.17), channel_id=1, source_target_pairs={{0,4},{4,8},{8,12},{12,16},{16,20},{20,24},{24,28},{28,0},{32,36},... | collective-permute-start | bytes 786440 | tf_op jit(solution)/shard_map/ppermute | solution.py:32
  82.0 9.5 %collective-permute-start.7 = (bf16[2,256,256]{2,1,0:T(8,128)(2,1)S(1)}, bf16[2,256,256]{2,1,0:T(8,128)(2,1)S(1)}, u32[]{:S(2)}, u32[]{:S(2)}) collective-permute-start(bf16[2,256,256]{2,1,0:T(8,128)(2,1)S(1)} %slice.18), channel_id=1, source_target_pairs={{0,28},{4,0},{8,4},{12,8},{16,12},{20,16},{24,20},{28,24},{32,60},... | collective-permute-start | bytes 786440 | tf_op jit(solution)/shard_map/ppermute | solution.py:32
  96.6 7.0 %copy-start.11 = (s32[129]{0:T(256)S(1)}, s32[129]{0:T(256)}, u32[]{:S(2)}) copy-start(s32[129]{0:T(256)} %flags.1.refs_0_.flag_ref) | copy-start | bytes 1552
  96.6 19.9 %all-to-all-start.2 = ((bf16[4,128,1152]{2,1,0:T(8,128)(2,1)}), bf16[4,128,1152]{2,1,0:T(8,128)(2,1)S(1)}, u32[]{:S(2)}, u32[]{:S(2)}) async-start(bf16[4,128,1152]{2,1,0:T(8,128)(2,1)} %shard_map.59), calls=%async_computation.2 | async-start | bytes 2359296 | tf_op jit(solution)/shard_map/all_to_all | solution.py:40
  103.7 1.0 copy-start.3
  104.7 1.0 copy-start.6
  105.8 1.0 copy-start.14
  115.8 0.7 copy-start.7
  116.5 2.2 %copy-start = (bf16[1024,2048]{1,0:T(8,128)(2,1)S(1)}, bf16[1024,2048]{1,0:T(8,128)(2,1)}, u32[]{:S(2)}) copy-start(bf16[1024,2048]{1,0:T(8,128)(2,1)} %w_ref.3) | copy-start | bytes 12582916
  118.7 1.0 copy-start.8
  119.7 12.7 %copy-start.1 = (bf16[1024,2048]{1,0:T(8,128)(2,1)S(1)}, bf16[1024,2048]{1,0:T(8,128)(2,1)}, u32[]{:S(2)}) copy-start(bf16[1024,2048]{1,0:T(8,128)(2,1)} %w_ref.3) | copy-start | bytes 12582916
  121.5 12.0 %collective-permute-start.8 = (bf16[2,128,512]{2,1,0:T(8,128)(2,1)S(1)}, bf16[2,128,512]{2,1,0:T(8,128)(2,1)S(1)}, u32[]{:S(2)}, u32[]{:S(2)}) collective-permute-start(bf16[2,128,512]{2,1,0:T(8,128)(2,1)S(1)} %get-tuple-element.20), channel_id=1, source_target_pairs={{0,1},{1,0},{2,3},{3,2},{4,5},{5,4},{6,7},{7,6},{8,9},{9,8},{10,11... | collective-permute-start | bytes 786440 | tf_op jit(solution)/shard_map/ppermute | solution.py:279
  133.6 10.6 %collective-permute-start.9 = (bf16[128,512]{1,0:T(8,128)(2,1)S(1)}, bf16[128,512]{1,0:T(8,128)(2,1)S(1)}, u32[]{:S(2)}, u32[]{:S(2)}) collective-permute-start(bf16[128,512]{1,0:T(8,128)(2,1)S(1)} %fusion.2), channel_id=1, source_target_pairs={{0,2},{1,3},{2,0},{3,1},{4,6},{5,7},{6,4},{7,5},{8,10},{9,11},{10,... | collective-permute-start | bytes 393224 | tf_op jit(solution)/shard_map/ppermute | solution.py:284
